TPU v7x, 256 devices: a whole 4x4x8 slice. The times are simulated.
256 devices in a mesh: wide: 64 (over x, z, core), narrow: 4 (over y).
Axes of the slice: x: 4, y: 4, z: 8, core: 2. Of those that a mesh axis runs over, the one named last changes fastest.
Arguments:
- a_blocks: float32 [49152, 128, 128], P(('wide', 'narrow')), may hold values from -0.8 to 0.8
- row_map: int32 [49152, 128], P(('wide', 'narrow')), may hold values from 0 to 127
- col_map: int32 [49152, 128], P(('wide', 'narrow')), may hold values from 0 to 127
- target: int32 [49152], P(('wide', 'narrow')), may hold values from 0 to 839
- counts: int32 [64], P('wide'), may hold values from 1 to 8, as said below
- weights: int32 [512], P('wide'), may hold values from 1 to 999
Outputs:
- coarse: float32 [512, 128, 128], P('wide', 'narrow')
- work_offset: int32 [512], P('wide')
Inputs may be any that keep to these rules, and one draw needn't show every extreme that they name: `counts`: every index of wide has at least one live slot and at most 8; some index has exactly 8; the last index has fewer than 8.
All inputs are finite; a program needn't handle non-finite values.
Results may differ from a plain program's by a relative error of at most 0.0003.
Values sent between devices are 32-bit elements; how exact they have to be, the bound alone decides.
A program may use at most 128 MiB of HBM per device.

v0:
```python
import jax
import jax.numpy as jnp
from jax import lax
from jax.sharding import PartitionSpec as P


def from_everyone(array, axis):
    devices = lax.axis_size(axis)
    return lax.all_to_all(
        jnp.broadcast_to(array[None], (devices, *array.shape)), axis, 0, 0, tiled=True
    )


def collected_together(array, axis):
    leaves = jax.tree.leaves(array)
    turns = sorted(range(len(leaves)), key=lambda k: -leaves[k].size)
    width = (1, *leaves[turns[0]].shape)[-1]
    lines = [
        jnp.pad(leaves[k].reshape(-1), (0, -leaves[k].size % width)).reshape(-1, width)
        for k in turns
    ]
    both, at, found = (from_everyone(jnp.concatenate(lines), axis), 0, {})
    for k, line in zip(turns, lines):
        piece = both[:, at : at + len(line)].reshape(len(both), -1)
        found[k] = piece[:, : leaves[k].size].reshape(-1, *leaves[k].shape)
        at += len(line)
    numbers = iter(range(len(leaves)))
    return jax.tree.map(lambda _: found[next(numbers)], array)


def folded_in_pairs(pieces, combine):
    while len(jax.tree.leaves(pieces)[0]) > 1:
        pieces = jax.vmap(combine)(
            *(jax.tree.map(lambda part: part[side::2], pieces) for side in (0, 1))
        )
    return jax.tree.map(lambda part: part[0], pieces)


def entering(array, axis, combine, identity):
    devices, place = (lax.axis_size(axis), lax.axis_index(axis))
    passed = jnp.arange(devices) > place

    def kept(part, zero, own):
        part = jnp.where(
            passed.reshape(-1, *(1 for _ in own.shape)), part, jnp.asarray(zero, own.dtype)
        )
        return part[::-1]

    pieces = collected_together(array, axis)
    return folded_in_pairs(jax.tree.map(kept, pieces, identity, array), combine)


def cut_along(array, dim, devices):
    shape = array.shape
    pieces = array.reshape(*shape[:dim], devices, shape[dim] // devices, *shape[dim + 1 :])
    return jnp.moveaxis(pieces, dim, 0)


def summed_on_arrival(array, axis, dim):
    pieces = cut_along(array, dim, lax.axis_size(axis))
    arrived = lax.all_to_all(pieces, axis, split_axis=0, concat_axis=0, tiled=True)
    return arrived.sum(axis=0)


def local(a_blocks, row_map, col_map, target, counts, weights):
    block_size = a_blocks.shape[1]
    slot_count = weights.shape[0]
    nwide = lax.axis_size("wide")
    own_index = lax.axis_index("wide")
    live_count = counts[0]
    slot_of = target % live_count
    target_positions = jnp.arange(slot_count, dtype=jnp.int32)
    is_live = target_positions < live_count
    live_weight = jnp.where(is_live, weights, 0)
    local_total = jnp.sum(live_weight)

    def combine(earlier, later):
        return (earlier[0] + later[0], earlier[1] + later[1])

    zero_one = jnp.zeros((1,), jnp.int32)
    higher_count, higher_weight = entering(
        (counts, local_total[None]), "wide", combine, (zero_one, zero_one)
    )
    higher_count = higher_count[0]
    higher_weight = higher_weight[0]
    start = (nwide * slot_count - higher_count - live_count).astype(jnp.int32)
    inner = jnp.arange(block_size, dtype=jnp.int32)
    row_onehot = (row_map[:, :, None] == inner[None, None, :]).astype(jnp.float32)
    col_onehot = (col_map[:, :, None] == inner[None, None, :]).astype(jnp.float32)
    merged = jnp.einsum("brc,bcd->brd", a_blocks, col_onehot, precision=lax.Precision.HIGHEST)
    reduced = jnp.einsum("bre,brd->bed", row_onehot, merged, precision=lax.Precision.HIGHEST)
    select = (slot_of[:, None] == target_positions[None, :]).astype(jnp.float32)
    partial_value = jnp.einsum("bs,bed->sed", select, reduced, precision=lax.Precision.HIGHEST)
    accumulated_sum = summed_on_arrival(partial_value, "narrow", 1)
    destination = jnp.where(is_live, start + target_positions, -1)
    offset_of = jnp.where(is_live, higher_weight + local_total - jnp.cumsum(live_weight), 0).astype(
        jnp.int32
    )

    def place(carry, piece, first_row):
        blocks_in, entry_index, offset_in = piece
        local_position = entry_index - own_index * slot_count
        pick = local_position[None, :] == target_positions[:, None]
        blocks_acc = jnp.einsum(
            "sk,kjm->sjm", pick.astype(jnp.float32), blocks_in, precision=lax.Precision.HIGHEST
        )
        offset_acc = jnp.sum(jnp.where(pick, offset_in[None, :], 0), axis=1).astype(jnp.int32)
        return (blocks_acc, offset_acc)

    starting_value = (jnp.zeros_like(accumulated_sum), jnp.zeros((slot_count,), jnp.int32))
    coarse, work_offset = place(
        starting_value,
        (
            lax.all_gather(accumulated_sum, "wide", axis=0, tiled=True),
            lax.all_gather(destination, "wide", axis=0, tiled=True),
            lax.all_gather(offset_of, "wide", axis=0, tiled=True),
        ),
        jnp.int32(0),
    )
    return (coarse, work_offset)


def solution(mesh):
    return jax.shard_map(
        local,
        mesh=mesh,
        in_specs=(
            P(("wide", "narrow"), None, None),
            P(("wide", "narrow"), None),
            P(("wide", "narrow"), None),
            P(("wide", "narrow")),
            P("wide"),
            P("wide"),
        ),
        out_specs=(P("wide", "narrow", None), P("wide")),
        check_vma=False,
    )
```

profile of v0, /device:TPU:1, one launch (start us, length us, event | category | flops | bytes accessed | tf_op | source)
XLA Modules:
  0.0 170.2 jit_solution(2894555940684232025)
XLA Ops:
  7.2 0.0 all-gather.2.cloned.1.call-start
  7.9 15.9 %fusion.3 = f32[192,128,128]{2,1,0:T(8,128)S(1)} fusion(f32[192,128,128]{2,1,0:T(8,128)} %param.6, s32[192,128]{1,0:T(8,128)} %param.8), kind=kOutput, calls=%fused_computation.5 | convolution fusion | flops 4834983936 | bytes 25264128 | tf_op jit(solution)/shard_map/brc,bcd->brd/dot_general | solution.py:90
  23.8 15.4 %fusion.2 = f32[192,128,128]{2,1,0:T(8,128)} fusion(f32[192,128,128]{2,1,0:T(8,128)S(1)} %fusion.3, s32[192,128]{1,0:T(8,128)S(1)} %copy-done), kind=kOutput, calls=%fused_computation.4 | convolution fusion | flops 4834983936 | bytes 25264128 | tf_op jit(solution)/shard_map/bre,brd->bed/dot_general | solution.py:91
  39.2 0.1 and_select_fusion
  39.4 15.4 %fusion = f32[8,128,128]{2,0,1:T(8,128)S(1)} fusion(f32[192,128,128]{2,1,0:T(8,128)} %fusion.2, s32[192]{0:T(256)S(1)} %and_select_fusion), kind=kOutput, calls=%fused_computation | convolution fusion | flops 301991424 | bytes 13107968 | tf_op jit(solution)/shard_map/bs,bed->sed/dot_general | solution.py:93
  54.8 13.4 %all_to_all.10 = f32[4,8,32,128]{3,1,2,0:T(8,128)S(1)} all-to-all(f32[4,8,32,128]{3,1,2,0:T(8,128)S(1)} %bitcast.37), channel_id=1, replica_groups=mesh['wide'=64,'narrow'=4] {'narrow'}, dimensions={0} | all-to-all | bytes 1048576 | tf_op jit(solution)/shard_map/all_to_all | solution.py:61
  68.2 0.7 reduce_sum.28
  68.9 0.6 fusion.15
  69.6 0.6 add_bitcast_fusion
  70.2 0.6 broadcast_in_dim.45
  70.8 13.3 %all-to-all-start = ((s32[64,2,1]{1,2,0:T(1,128)}), s32[64,2,1]{1,2,0:T(1,128)S(1)}, u32[]{:S(2)}, u32[]{:S(2)}) async-start(s32[64,2,1]{1,2,0:T(1,128)} %broadcast_in_dim.45), calls=%async_computation | async-start | bytes 65536 | tf_op jit(solution)/shard_map/all_to_all | solution.py:9
  84.1 0.6 dynamic-slice
  85.2 0.2 reduce-window.9
  85.4 8.1 %all-to-all-done = s32[64,2,1]{1,2,0:T(1,128)S(1)} async-done(((s32[64,2,1]{1,2,0:T(1,128)}), s32[64,2,1]{1,2,0:T(1,128)S(1)}, u32[]{:S(2)}, u32[]{:S(2)}) %all-to-all-start) | async-done | bytes 544 | tf_op jit(solution)/shard_map/all_to_all | solution.py:9
  93.5 2.4 %slice_reduce_fusion = (s32[64]{0:T(128)S(1)}, s32[64]{0:T(128)S(1)}) fusion(s32[64,2,1]{1,2,0:T(1,128)S(1)} %all-to-all-done), kind=kLoop, calls=%fused_computation.8 | loop fusion | bytes 1024 | tf_op jit(solution)/shard_map/slice | solution.py:24
  96.0 0.1 slice.95
  96.1 0.1 slice.97
  96.2 0.1 slice.96
  96.3 0.1 slice.98
  96.4 0.1 slice.99
  96.5 0.1 slice.100
  96.6 0.1 slice.101
  96.7 0.1 slice.102
  96.8 0.1 slice.103
  96.9 0.1 slice.104
  97.0 0.1 slice.105
  97.1 0.1 slice.106
  97.2 0.1 slice.110
  97.4 0.1 slice.112
  97.5 0.1 slice.111
  97.6 0.1 slice.113
  97.7 0.1 slice.114
  97.8 0.1 slice.115
  97.9 0.1 slice.116
  98.0 0.1 slice.117
  98.1 0.1 slice.118
  98.2 0.1 slice.119
  98.3 0.1 slice.120
  98.4 0.1 slice.121
  98.5 0.6 fusion.17
  101.0 0.6 fusion.18
  102.7 0.1 select_dynamic-update-slice_fusion
  102.8 0.1 fusion.13
  102.9 13.4 %all-reduce.2 = (s32[512]{0:T(512)S(1)}, s32[512]{0:T(512)S(1)}) all-reduce(s32[512]{0:T(512)S(1)} %select_dynamic-update-slice_fusion, s32[512]{0:T(512)S(1)} %fusion.13), channel_id=1, replica_groups=mesh['wide'=64,'narrow'=4] {'wide'}, use_global_device_ids=true, to_apply=%add | all-reduce | flops 1024 | bytes 8192
  116.4 0.6 select_reduce_fusion
  117.0 39.5 %all-gather.2.cloned.1.call-done = f32[512,32,128]{2,0,1:T(8,128)} async-done(((f32[8,32,128]{2,0,1:T(8,128)}), f32[512,32,128]{2,0,1:T(8,128)}) %all-gather.2.cloned.1.call-update) | async-done | bytes 8388624 | tf_op jit(solution)/shard_map/all_gather | solution.py:114
  156.5 6.2 %fusion.7 = f32[8,32,128]{2,0,1:T(8,128)S(1)} fusion(f32[512,32,128]{2,0,1:T(8,128)} %all-gather.2.cloned.1.call-done, s32[512]{0:T(512)S(1)} %broadcast_subtract_fusion), kind=kOutput, calls=%fused_computation.13 | convolution fusion | flops 201330688 | bytes 8521728 | tf_op jit(solution)/shard_map/sk,kjm->sjm/dot_general | solution.py:104
  162.7 0.7 copy.13
  (23 shorter events, 0.1 us)
Async XLA Ops:
  7.2 149.3 %all-gather.2.cloned.1.call-start = ((), (), s32[]{:S(2)}) async-start(), calls=%async_computation.2 | async-start | bytes 8519680 | tf_op jit(solution)/shard_map/all_gather | solution.py:114
  7.9 15.9 %copy-start = (s32[192,128]{1,0:T(8,128)S(1)}, s32[192,128]{1,0:T(8,128)}, u32[]{:S(2)}) copy-start(s32[192,128]{1,0:T(8,128)} %param.7) | copy-start | bytes 294916
  23.8 15.4 %copy-start.1 = (s32[192]{0:T(256)S(1)}, s32[192]{0:T(256)}, u32[]{:S(2)}) copy-start(s32[192]{0:T(256)} %param.9) | copy-start | bytes 2308
  39.2 29.7 %copy-start.2 = (s32[8]{0:T(128)S(1)}, s32[8]{0:T(128)}, u32[]{:S(2)}) copy-start(s32[8]{0:T(128)} %param.11) | copy-start | bytes 100
  39.2 44.9 %copy-start.3 = (u32[256]{0:T(256)S(1)}, u32[256]{0:T(256)}, u32[]{:S(2)}) copy-start(u32[256]{0:T(256)} %constant.37) | copy-start | bytes 3076
  70.8 22.7 %all-to-all-start = ((s32[64,2,1]{1,2,0:T(1,128)}), s32[64,2,1]{1,2,0:T(1,128)S(1)}, u32[]{:S(2)}, u32[]{:S(2)}) async-start(s32[64,2,1]{1,2,0:T(1,128)} %broadcast_in_dim.45), calls=%async_computation | async-start | bytes 65536 | tf_op jit(solution)/shard_map/all_to_all | solution.py:9
Sparse Core Ops, SparseCore 0:
  69.0 87.4 all-gather.1
where the time goes:
time: 171 us; the launch traced here: 170 us
  matrix products  52.9 us (31%)
  waiting for transfers between devices  47.6 us (28%)
  blocking collectives  26.9 us (16%)
  between operations  18.4 us (11%)
  starting transfers between devices  13.3 us (8%)
  local copies, waits for them, and re-layouts  7.94 us (5%)
  other arithmetic  3.17 us (2%)
    all_gather x1, waiting for transfers between devices, local(): lax.all_gather(accumulated_sum, 'wide', axis=0, tiled=True)  39.5 us
    dot_general x1, matrix products, local(): jnp.einsum('brc,bcd->brd', a_blocks, col_onehot, precision=lax.Precision....  15.9 us
    dot_general x1, matrix products, local(): jnp.einsum('bre,brd->bed', row_onehot, merged, precision=lax.Precision.HI...  15.4 us
    dot_general x1, matrix products, local(): jnp.einsum('bs,bed->sed', select, reduced, precision=lax.Precision.HIGHEST)  15.4 us
    unnamed x1, blocking collectives  13.4 us
    all_to_all x1, blocking collectives, summed_on_arrival(): lax.all_to_all(pieces, axis, split_axis=0, concat_axis=0, tiled=True)  13.4 us
    all_to_all x1, starting transfers between devices, from_everyone(): lax.all_to_all(jnp.broadcast_to(array[None], (devices, *array.shape)), ax...  13.3 us
    all_to_all x1, waiting for transfers between devices, from_everyone(): lax.all_to_all(jnp.broadcast_to(array[None], (devices, *array.shape)), ax...  8.08 us
  transfers between devices with their start and end apart: 2, of which 2 were waited for; matrix products, arithmetic and copies ran while one was open for 6% of the time, Pallas kernels for 0%

commit v1 on v0

--- a/solution.py
+++ b/solution.py
@@ -1,7 +1,79 @@
+import functools
+
 import jax
 import jax.numpy as jnp
 from jax import lax
+from jax.experimental import pallas as pl
+from jax.experimental.pallas import tpu as pltpu
 from jax.sharding import PartitionSpec as P
+
+BLOCK = 128
+GROUP = 16
+
+
+def split(value):
+    high = value.astype(jnp.bfloat16)
+    return high, (value - high.astype(jnp.float32)).astype(jnp.bfloat16)
+
+
+def reduced_block(a, row, col, sublane):
+    one, zero = jnp.float32(1), jnp.float32(0)
+    pick_row = jnp.where(sublane == row, one, zero).astype(jnp.bfloat16)
+    pick_col = jnp.where(sublane == col, one, zero).astype(jnp.bfloat16)
+    merged = jnp.dot(
+        jnp.concatenate([pick_row, pick_row], 1),
+        jnp.concatenate(split(a), 0),
+        preferred_element_type=jnp.float32,
+    )
+    return lax.dot_general(
+        jnp.concatenate(split(merged), 1),
+        jnp.concatenate([pick_col, pick_col], 1),
+        (((1,), (1,)), ((), ())),
+        preferred_element_type=jnp.float32,
+    )
+
+
+def partial_kernel(target, counts, a_hbm, row_map, col_map, out, a_vmem, arrived):
+    steps = a_hbm.shape[0] // GROUP
+
+    def copy(i):
+        part = pl.ds(i * GROUP, GROUP)
+        return pltpu.make_async_copy(a_hbm.at[part], a_vmem.at[part], arrived.at[i])
+
+    for i in range(steps):
+        copy(i).start()
+    out[...] = jnp.zeros_like(out)
+    live = counts[0]
+    sublane = lax.broadcasted_iota(jnp.int32, (BLOCK, BLOCK), 0)
+
+    def step(i, carry):
+        copy(i).wait()
+        for j in range(GROUP):
+            b = i * GROUP + j
+            out[lax.rem(target[b], live)] += reduced_block(
+                a_vmem[b], row_map[pl.ds(b, 1), :], col_map[pl.ds(b, 1), :], sublane
+            )
+        return carry
+
+    lax.fori_loop(0, steps, step, 0)
+
+
+def partial_sums(a_blocks, row_map, col_map, target, counts, slots):
+    n = a_blocks.shape[0]
+    smem = pl.BlockSpec(memory_space=pltpu.SMEM)
+    vmem = pl.BlockSpec(memory_space=pltpu.VMEM)
+    return pl.pallas_call(
+        partial_kernel,
+        out_shape=jax.ShapeDtypeStruct((slots, BLOCK, BLOCK), jnp.float32),
+        in_specs=[smem, smem, pl.BlockSpec(memory_space=pl.ANY), vmem, vmem],
+        out_specs=vmem,
+        scratch_shapes=[
+            pltpu.VMEM((n, BLOCK, BLOCK), jnp.float32),
+            pltpu.SemaphoreType.DMA((n // GROUP,)),
+        ],
+        cost_estimate=pl.CostEstimate(flops=n * 8 * BLOCK**3, bytes_accessed=n * BLOCK * BLOCK * 4, transcendentals=0),
+        name="partial_sums",
+    )(target, counts, a_blocks, row_map, col_map)
 
 
 def from_everyone(array, axis):
@@ -63,12 +135,10 @@
 
 
 def local(a_blocks, row_map, col_map, target, counts, weights):
-    block_size = a_blocks.shape[1]
     slot_count = weights.shape[0]
     nwide = lax.axis_size("wide")
     own_index = lax.axis_index("wide")
     live_count = counts[0]
-    slot_of = target % live_count
     target_positions = jnp.arange(slot_count, dtype=jnp.int32)
     is_live = target_positions < live_count
     live_weight = jnp.where(is_live, weights, 0)
@@ -84,13 +154,7 @@
     higher_count = higher_count[0]
     higher_weight = higher_weight[0]
     start = (nwide * slot_count - higher_count - live_count).astype(jnp.int32)
-    inner = jnp.arange(block_size, dtype=jnp.int32)
-    row_onehot = (row_map[:, :, None] == inner[None, None, :]).astype(jnp.float32)
-    col_onehot = (col_map[:, :, None] == inner[None, None, :]).astype(jnp.float32)
-    merged = jnp.einsum("brc,bcd->brd", a_blocks, col_onehot, precision=lax.Precision.HIGHEST)
-    reduced = jnp.einsum("bre,brd->bed", row_onehot, merged, precision=lax.Precision.HIGHEST)
-    select = (slot_of[:, None] == target_positions[None, :]).astype(jnp.float32)
-    partial_value = jnp.einsum("bs,bed->sed", select, reduced, precision=lax.Precision.HIGHEST)
+    partial_value = partial_sums(a_blocks, row_map, col_map, target, counts, slot_count)
     accumulated_sum = summed_on_arrival(partial_value, "narrow", 1)
     destination = jnp.where(is_live, start + target_positions, -1)
     offset_of = jnp.where(is_live, higher_weight + local_total - jnp.cumsum(live_weight), 0).astype(

time: 171 us -> 138 us (0.81)
  matrix products: 52.9 us -> 6.18 us
  Pallas kernels: 0 us -> 12.8 us
  local copies, waits for them, and re-layouts: 7.94 us -> 9.75 us
    dot_general x3 -> x0, matrix products: 46.8 us -> none  [the longest x1 15.9 us: local(): jnp.einsum('brc,bcd->brd', a_blocks, col_onehot, precision=lax.Precision....]
    pallas_call x0 -> x1, Pallas kernels: none -> 12.8 us  [partial_sums(): pl.pallas_call(partial_kernel, out_shape=jax.ShapeDtypeStruct((slots, BLO...]
  transfers between devices with their start and end apart: 2 -> 2, of which waited for: 2 -> 2; matrix products, arithmetic and copies ran while one was open for 6% -> 7% of each run, Pallas kernels for 0% -> 0%
where the time goes in v1:
time: 138 us; the launch traced here: 137 us
  waiting for transfers between devices  47.6 us (34%)
  blocking collectives  26.9 us (19%)
  between operations  18.4 us (13%)
  starting transfers between devices  13.3 us (10%)
  Pallas kernels  12.8 us (9%)
  local copies, waits for them, and re-layouts  9.75 us (7%)
  matrix products  6.18 us (4%)
  other arithmetic  2.4 us (2%)
    all_gather x1, waiting for transfers between devices, local(): lax.all_gather(accumulated_sum, 'wide', axis=0, tiled=True)  39.5 us
    unnamed x1, blocking collectives  13.5 us
    all_to_all x1, blocking collectives, summed_on_arrival(): lax.all_to_all(pieces, axis, split_axis=0, concat_axis=0, tiled=True)  13.4 us
    all_to_all x1, starting transfers between devices, from_everyone(): lax.all_to_all(jnp.broadcast_to(array[None], (devices, *array.shape)), ax...  13.3 us
    pallas_call x1, Pallas kernels, partial_sums(): pl.pallas_call(partial_kernel, out_shape=jax.ShapeDtypeStruct((slots, BLO...  12.8 us
    all_to_all x1, waiting for transfers between devices, from_everyone(): lax.all_to_all(jnp.broadcast_to(array[None], (devices, *array.shape)), ax...  8.09 us
    dot_general x1, matrix products, place(): jnp.einsum('sk,kjm->sjm', pick.astype(jnp.float32), blocks_in, precision=...  6.18 us
    slice x26, local copies, waits for them, and re-layouts, folded_in_pairs(): part[side::2]  3.64 us
  transfers between devices with their start and end apart: 2, of which 2 were waited for; matrix products, arithmetic and copies ran while one was open for 7% of the time, Pallas kernels for 0%

profile of v1, /device:TPU:1, one launch (start us, length us, event | category | flops | bytes accessed | tf_op | source)
XLA Modules:
  0.0 137.2 jit_solution(2750447771630490043)
XLA Ops:
  7.2 0.0 copy-start.1
  7.2 0.0 all-gather.2.cloned.1.call-start
  7.9 12.8 %partial_sums.1 = f32[8,128,128]{2,1,0:T(8,128)} custom-call(s32[192]{0:T(256)} %target.1, s32[1]{0:T(128)} %copy.27.counts, f32[192,128,128]{2,1,0:T(8,128)} %a_hbm.1, s32[192,128]{1,0:T(8,128)} %row_map.1, s32[192,128]{1,0:T(8,128)} %col_map.1), custom_call_target="tpu_custom_call" | custom-call | flops 3221225472 | bytes 12582912 | tf_op jit(solution)/shard_map/partial_sums/pallas_call | solution.py:65
  20.6 1.1 copy.23
  21.7 13.4 %all_to_all.10 = f32[4,8,32,128]{3,2,1,0:T(8,128)S(1)} all-to-all(f32[4,8,32,128]{3,2,1,0:T(8,128)S(1)} %bitcast.32), channel_id=1, replica_groups=mesh['wide'=64,'narrow'=4] {'narrow'}, dimensions={0} | all-to-all | bytes 1048576 | tf_op jit(solution)/shard_map/all_to_all | solution.py:133
  35.2 0.7 copy.19
  35.9 0.0 all-gather.2.cloned.1.call-update
  36.0 0.6 fusion.6
  36.6 0.6 add_bitcast_fusion
  37.2 0.6 broadcast_in_dim.39
  37.9 13.3 %all-to-all-start = ((s32[64,2,1]{1,2,0:T(1,128)}), s32[64,2,1]{1,2,0:T(1,128)S(1)}, u32[]{:S(2)}, u32[]{:S(2)}) async-start(s32[64,2,1]{1,2,0:T(1,128)} %broadcast_in_dim.39), calls=%async_computation | async-start | bytes 65536 | tf_op jit(solution)/shard_map/all_to_all | solution.py:81
  51.2 0.6 dynamic-slice
  52.3 0.2 reduce-window.9
  52.5 8.1 %all-to-all-done = s32[64,2,1]{1,2,0:T(1,128)S(1)} async-done(((s32[64,2,1]{1,2,0:T(1,128)}), s32[64,2,1]{1,2,0:T(1,128)S(1)}, u32[]{:S(2)}, u32[]{:S(2)}) %all-to-all-start) | async-done | bytes 544 | tf_op jit(solution)/shard_map/all_to_all | solution.py:81
  60.6 2.4 %slice_reduce_fusion = (s32[64]{0:T(128)S(1)}, s32[64]{0:T(128)S(1)}) fusion(s32[64,2,1]{1,2,0:T(1,128)S(1)} %all-to-all-done), kind=kLoop, calls=%fused_computation.1 | loop fusion | bytes 1024 | tf_op jit(solution)/shard_map/slice | solution.py:96
  63.0 0.1 slice.112
  63.1 0.1 slice.110
  63.3 0.1 slice.111
  63.3 0.1 slice.113
  63.4 0.1 slice.115
  63.6 0.1 slice.114
  63.7 0.1 slice.117
  63.8 0.1 slice.116
  63.9 0.1 slice.119
  64.0 0.1 slice.118
  64.1 0.1 slice.121
  64.2 0.1 slice.120
  64.3 0.1 slice.97
  64.4 0.1 slice.95
  64.5 0.1 slice.96
  64.6 0.1 slice.98
  64.7 0.1 slice.100
  64.8 0.1 slice.99
  65.0 0.1 slice.102
  65.1 0.1 slice.101
  65.2 0.1 slice.104
  65.3 0.1 slice.103
  65.4 0.1 slice.106
  65.5 0.1 slice.105
  65.6 0.6 fusion.8
  68.0 0.6 fusion.9
  69.8 0.1 select_dynamic-update-slice_fusion
  69.9 0.1 fusion.4
  70.0 13.5 %all-reduce.2 = (s32[512]{0:T(512)S(1)}, s32[512]{0:T(512)S(1)}) all-reduce(s32[512]{0:T(512)S(1)} %select_dynamic-update-slice_fusion, s32[512]{0:T(512)S(1)} %fusion.4), channel_id=1, replica_groups=mesh['wide'=64,'narrow'=4] {'wide'}, use_global_device_ids=true, to_apply=%add | all-reduce | flops 1024 | bytes 8192
  83.4 0.6 select_reduce_fusion
  84.1 39.5 %all-gather.2.cloned.1.call-done = f32[512,32,128]{2,0,1:T(8,128)} async-done(((f32[8,32,128]{2,0,1:T(8,128)}), f32[512,32,128]{2,0,1:T(8,128)}) %all-gather.2.cloned.1.call-update) | async-done | bytes 8388624 | tf_op jit(solution)/shard_map/all_gather | solution.py:178
  123.5 6.2 %fusion.1 = f32[8,32,128]{2,0,1:T(8,128)S(1)} fusion(f32[512,32,128]{2,0,1:T(8,128)} %all-gather.2.cloned.1.call-done, s32[512]{0:T(512)S(1)} %broadcast_subtract_fusion), kind=kOutput, calls=%fused_computation.6 | convolution fusion | flops 201330688 | bytes 8521728 | tf_op jit(solution)/shard_map/sk,kjm->sjm/dot_general | solution.py:168
  129.7 0.7 copy.20
  (18 shorter events, 0.1 us)
Async XLA Ops:
  7.2 44.0 %copy-start.1 = (u32[256]{0:T(256)S(1)}, u32[256]{0:T(256)}, u32[]{:S(2)}) copy-start(u32[256]{0:T(256)} %constant.30) | copy-start | bytes 3076
  7.2 28.8 %copy-start = (s32[8]{0:T(128)S(1)}, s32[8]{0:T(128)}, u32[]{:S(2)}) copy-start(s32[8]{0:T(128)} %param.11) | copy-start | bytes 100
  7.2 116.3 %all-gather.2.cloned.1.call-start = ((), (), s32[]{:S(2)}) async-start(), calls=%async_computation.2 | async-start | bytes 8519680 | tf_op jit(solution)/shard_map/all_gather | solution.py:178
  37.9 22.7 %all-to-all-start = ((s32[64,2,1]{1,2,0:T(1,128)}), s32[64,2,1]{1,2,0:T(1,128)S(1)}, u32[]{:S(2)}, u32[]{:S(2)}) async-start(s32[64,2,1]{1,2,0:T(1,128)} %broadcast_in_dim.39), calls=%async_computation | async-start | bytes 65536 | tf_op jit(solution)/shard_map/all_to_all | solution.py:81
Sparse Core Ops, SparseCore 0:
  36.1 87.4 all-gather.1

commit v2 on v1

v2 whole, which is shorter than its diff:
```python
import functools

import jax
import jax.numpy as jnp
from jax import lax
from jax.experimental import pallas as pl
from jax.experimental.pallas import tpu as pltpu
from jax.sharding import PartitionSpec as P

BLOCK = 128
GROUP = 16
SLOTS = 8
WIDE = 64
NARROW = 4
CHIPS = WIDE // 2
Z = 8
X = CHIPS // Z
ROWS = BLOCK // NARROW
HALF = SLOTS // 2
F32 = jnp.float32
I32 = jnp.int32
BF16 = jnp.bfloat16


def split(value):
    high = value.astype(BF16)
    return high, (value - high.astype(F32)).astype(BF16)


def reduced_block(a, row, col, sublane):
    one, zero = F32(1), F32(0)
    pick_row = jnp.where(sublane == row, one, zero).astype(BF16)
    pick_col = jnp.where(sublane == col, one, zero).astype(BF16)
    merged = jnp.dot(
        jnp.concatenate([pick_row, pick_row], 1),
        jnp.concatenate(split(a), 0),
        preferred_element_type=F32,
    )
    return lax.dot_general(
        jnp.concatenate(split(merged), 1),
        jnp.concatenate([pick_col, pick_col], 1),
        (((1,), (1,)), ((), ())),
        preferred_element_type=F32,
    )


def partial_kernel(target, counts, a_hbm, row_map, col_map, out, a_vmem, arrived):
    steps = a_hbm.shape[0] // GROUP

    def copy(i):
        part = pl.ds(i * GROUP, GROUP)
        return pltpu.make_async_copy(a_hbm.at[part], a_vmem.at[part], arrived.at[i])

    for i in range(steps):
        copy(i).start()
    out[...] = jnp.zeros_like(out)
    live = counts[0]
    sublane = lax.broadcasted_iota(I32, (BLOCK, BLOCK), 0)

    def step(i, carry):
        copy(i).wait()
        for j in range(GROUP):
            b = i * GROUP + j
            out[lax.rem(target[b], live)] += reduced_block(
                a_vmem[b], row_map[pl.ds(b, 1), :], col_map[pl.ds(b, 1), :], sublane
            )
        return carry

    lax.fori_loop(0, steps, step, 0)


def partial_sums(a_blocks, row_map, col_map, target, counts):
    n = a_blocks.shape[0]
    smem = pl.BlockSpec(memory_space=pltpu.SMEM)
    vmem = pl.BlockSpec(memory_space=pltpu.VMEM)
    return pl.pallas_call(
        partial_kernel,
        out_shape=jax.ShapeDtypeStruct((SLOTS, BLOCK, BLOCK), F32),
        in_specs=[smem, smem, pl.BlockSpec(memory_space=pl.ANY), vmem, vmem],
        out_specs=vmem,
        scratch_shapes=[
            pltpu.VMEM((n, BLOCK, BLOCK), F32),
            pltpu.SemaphoreType.DMA((n // GROUP,)),
        ],
        name="partial_sums",
    )(target, counts, a_blocks, row_map, col_map)


def place_kernel(
    counts, weights, partial, coarse, offset,
    meta_own, meta, via_up, via_down, send_up, send_down, from_down, from_up,
    rows_out, rows_in, pick, placed, back, note_own, note_in,
    y_sent, y_got, meta_sent, meta_got, out_sent, out_got, back_sent, back_got, note_sent, note_got,
):
    w = lax.axis_index("wide")
    y = lax.axis_index("narrow")
    core = lax.rem(w, 2)
    chip = lax.div(w, 2)
    x = lax.div(chip, Z)
    z = lax.rem(chip, Z)
    up, down = lax.rem(y + 1, NARROW), lax.rem(y + NARROW - 1, NARROW)
    far = lax.rem(y + 2, NARROW)

    def remote(src, dst, sent, got, wide, narrow):
        return pltpu.make_async_remote_copy(
            src_ref=src, dst_ref=dst, send_sem=sent, recv_sem=got,
            device_id={"wide": wide, "narrow": narrow},
            device_id_type=pl.DeviceIdType.MESH,
        )

    barrier = pltpu.get_barrier_semaphore()
    for other in (up, down):
        pl.semaphore_signal(barrier, inc=1, device_id={"wide": w, "narrow": other},
                            device_id_type=pl.DeviceIdType.MESH)

    def greet(d, carry):
        pl.semaphore_signal(barrier, inc=1, device_id={"wide": lax.rem(w + d, WIDE), "narrow": y},
                            device_id_type=pl.DeviceIdType.MESH)
        return carry

    lax.fori_loop(1, WIDE, greet, 0)

    lane = lax.broadcasted_iota(I32, (1, BLOCK), 1)
    turn = lax.rem(lane, SLOTS)
    weight_row = jnp.zeros((1, BLOCK), I32)
    for s in range(SLOTS):
        weight_row = jnp.where(turn == s, weights[s], weight_row)
    meta_own[:, :BLOCK] = jnp.full((1, BLOCK), counts[0], I32)
    meta_own[:, BLOCK:] = weight_row
    pl.semaphore_wait(barrier, WIDE + 1)

    def piece(half, owner):
        return partial.at[pl.ds(half * HALF, HALF), pl.ds(owner * ROWS, ROWS), :]

    def y_copy(k):
        src, dst, narrow = (
            (piece(0, far), via_up, up),
            (piece(1, far), via_down, down),
            (piece(1, up), from_down.at[pl.ds(HALF, HALF)], up),
            (piece(0, down), from_up.at[pl.ds(0, HALF)], down),
            (send_up, from_down.at[pl.ds(0, HALF)], up),
            (send_down, from_up.at[pl.ds(HALF, HALF)], down),
        )[k]
        return remote(src, dst, y_sent.at[k], y_got.at[k], w, narrow)

    for k in range(4):
        y_copy(k).start()

    def each_chip(body):
        def visit(d, carry):
            dx = lax.rem(X // 2 + lax.div(d, Z), X)
            dz = lax.rem(Z // 2 + lax.rem(d, Z), Z)
            there = lax.rem(x + dx, X) * Z + lax.rem(z + dz, Z)

            @pl.when((there != chip) | (core == 0))
            def _():
                body(there)

            return carry

        lax.fori_loop(0, CHIPS, visit, 0)

    each_chip(lambda there: remote(
        meta_own, meta.at[w], meta_sent, meta_got, 2 * there + 1, y).start())

    y_copy(0).wait_recv()
    send_up[...] = via_up[...] + partial[pl.ds(0, HALF), pl.ds(up * ROWS, ROWS), :]
    y_copy(4).start()
    y_copy(1).wait_recv()
    send_down[...] = via_down[...] + partial[pl.ds(HALF, HALF), pl.ds(down * ROWS, ROWS), :]
    y_copy(5).start()

    @pl.when(core == 1)
    def _():
        meta[w] = meta_own[...]
        remote(meta.at[pl.ds(0, WIDE - 1)], meta.at[pl.ds(0, WIDE - 1)], meta_sent, meta_got, w - 1, y).wait_recv()
        total = WIDE * SLOTS
        entry = lax.broadcasted_iota(I32, (WIDE, total), 1)
        device = lax.broadcasted_iota(I32, (WIDE, total), 0)
        count = jnp.concatenate([meta[:, 0, :BLOCK]] * (total // BLOCK), 1).astype(F32)
        weight = jnp.concatenate([meta[:, 0, BLOCK:]] * (total // BLOCK), 1).astype(F32)
        owner = lax.div(entry, SLOTS)
        mine = device == owner
        zero = jnp.zeros_like(count)
        count_row = jnp.sum(jnp.where(mine, count, zero), 0, keepdims=True)
        weight_of = jnp.sum(jnp.where(mine, weight, zero), 0, keepdims=True)
        higher = jnp.sum(jnp.where(device >= owner, count, zero), 0, keepdims=True)
        slot = lax.rem(lax.broadcasted_iota(I32, (1, total), 1), SLOTS).astype(F32)
        live = slot < count_row
        goes_to = jnp.where(live, F32(total) - higher + slot, F32(-1))
        first = F32(total) - jnp.max(higher, 1, keepdims=True)
        wide_rows = lax.broadcasted_iota(I32, (total, total), 0).astype(F32)
        pick[...] = jnp.where(wide_rows == goes_to, F32(1), F32(0)).astype(BF16)
        for k in range(2):
            index = (lax.broadcasted_iota(I32, (SLOTS, total), 0) + (2 * chip + k) * SLOTS).astype(F32)
            above = jnp.sum(jnp.where(goes_to > index, weight_of, F32(0)), 1, keepdims=True)
            above = jnp.where(index[:, :1] >= first, above, F32(0))
            diagonal = lax.broadcasted_iota(I32, (SLOTS, BLOCK), 0) == lax.broadcasted_iota(I32, (SLOTS, BLOCK), 1)
            line = jnp.sum(jnp.where(diagonal, above, F32(0)), 0, keepdims=True).astype(I32)
            if k == 0:
                note_own[...] = line
            else:
                offset[...] = line[:, :SLOTS]
        note = remote(note_own, note_in, note_sent, note_got, w - 1, y)
        note.start()

    for k in (2, 3, 4, 5):
        y_copy(k).wait_recv()
    for s in range(SLOTS):
        rows_out[:, s, :] = (
            partial[s, pl.ds(y * ROWS, ROWS), :] + from_down[s] + from_up[s]
        )

    each_chip(lambda there: remote(
        rows_out.at[there], rows_in.at[w], out_sent, out_got, 2 * there + 1, y).start())

    @pl.when(core == 1)
    def _():
        rows_in[w] = rows_out[chip]
        most = rows_in.at[pl.ds(0, WIDE - 1)]
        remote(most, most, out_sent, out_got, w - 1, y).wait_recv()
        high, low = split(rows_in[...].reshape(WIDE * SLOTS, BLOCK))
        both = jnp.dot(pick[...], jnp.concatenate([high, low], 1), preferred_element_type=F32)
        placed[...] = (both[:, :BLOCK] + both[:, BLOCK:]).reshape(WIDE, SLOTS, BLOCK)
        back[chip] = placed[w]

        def deliver(d, carry):
            there = lax.rem(w + d, WIDE)
            remote(placed.at[there], back.at[chip], back_sent, back_got, there, y).start()
            return carry

        lax.fori_loop(1, WIDE, deliver, 0)
        few = back.at[pl.ds(0, CHIPS - 1)]
        remote(few, few, back_sent, back_got, w - 1, y).wait_recv()

    @pl.when(core == 0)
    def _():
        remote(back, back, back_sent, back_got, w + 1, y).wait_recv()
        remote(note_in, note_in, note_sent, note_got, w + 1, y).wait_recv()
        offset[...] = note_in[:, :SLOTS]

    for s in range(SLOTS):
        coarse[s] = back[:, s, :]

    for k in range(6):
        y_copy(k).wait_send()

    @pl.when(core == 1)
    def _():
        remote(note_own, note_in, note_sent, note_got, w - 1, y).wait_send()
        most = placed.at[pl.ds(0, WIDE - 1)]
        remote(most, most, back_sent, back_got, w - 1, y).wait_send()
        few = rows_out.at[pl.ds(0, CHIPS - 1)]
        remote(few, few, out_sent, out_got, w - 1, y).wait_send()
        some = meta.at[pl.ds(0, CHIPS - 1)]
        remote(some, some, meta_sent, meta_got, w - 1, y).wait_send()

    @pl.when(core == 0)
    def _():
        remote(rows_out, rows_out, out_sent, out_got, w + 1, y).wait_send()
        some = meta.at[pl.ds(0, CHIPS)]
        remote(some, some, meta_sent, meta_got, w + 1, y).wait_send()


def placed_blocks(counts, weights, partial):
    smem = pl.BlockSpec(memory_space=pltpu.SMEM)
    vmem = pl.BlockSpec(memory_space=pltpu.VMEM)
    dma = pltpu.SemaphoreType.DMA
    return pl.pallas_call(
        place_kernel,
        out_shape=(
            jax.ShapeDtypeStruct((SLOTS, ROWS, BLOCK), F32),
            jax.ShapeDtypeStruct((1, SLOTS), I32),
        ),
        in_specs=[smem, smem, vmem],
        out_specs=(vmem, vmem),
        scratch_shapes=[
            pltpu.VMEM((1, 2 * BLOCK), I32),
            pltpu.VMEM((WIDE, 1, 2 * BLOCK), I32),
            pltpu.VMEM((HALF, ROWS, BLOCK), F32),
            pltpu.VMEM((HALF, ROWS, BLOCK), F32),
            pltpu.VMEM((HALF, ROWS, BLOCK), F32),
            pltpu.VMEM((HALF, ROWS, BLOCK), F32),
            pltpu.VMEM((SLOTS, ROWS, BLOCK), F32),
            pltpu.VMEM((SLOTS, ROWS, BLOCK), F32),
            pltpu.VMEM((CHIPS, SLOTS, BLOCK), F32),
            pltpu.VMEM((WIDE, SLOTS, BLOCK), F32),
            pltpu.VMEM((WIDE * SLOTS, WIDE * SLOTS), BF16),
            pltpu.VMEM((WIDE, SLOTS, BLOCK), F32),
            pltpu.VMEM((CHIPS, SLOTS, BLOCK), F32),
            pltpu.VMEM((1, BLOCK), I32),
            pltpu.VMEM((1, BLOCK), I32),
            dma((6,)), dma((6,)),
            dma, dma, dma, dma, dma, dma, dma, dma,
        ],
        compiler_params=pltpu.CompilerParams(collective_id=0, has_side_effects=True),
        name="placed_blocks",
    )(counts, weights, partial)


def local(a_blocks, row_map, col_map, target, counts, weights):
    partial = partial_sums(a_blocks, row_map, col_map, target, counts)
    coarse, offset = placed_blocks(counts, weights, partial)
    return coarse, offset.reshape(SLOTS)


def solution(mesh):
    return jax.shard_map(
        local,
        mesh=mesh,
        in_specs=(
            P(("wide", "narrow"), None, None),
            P(("wide", "narrow"), None),
            P(("wide", "narrow"), None),
            P(("wide", "narrow")),
            P("wide"),
            P("wide"),
        ),
        out_specs=(P("wide", "narrow", None), P("wide")),
        check_vma=False,
    )
```

time: 138 us -> 51.8 us (0.38)
  waiting for transfers between devices: 47.6 us -> 0 us
  Pallas kernels: 12.8 us -> 47.6 us
  blocking collectives: 26.9 us -> 0 us
  between operations: 18.4 us -> 1.29 us
  starting transfers between devices: 13.3 us -> 0 us
  local copies, waits for them, and re-layouts: 9.75 us -> 2.74 us
  matrix products: 6.18 us -> 0 us
  other arithmetic: 2.4 us -> 0 us
    all_gather x1 -> x0, waiting for transfers between devices: 39.5 us -> none  [local(): lax.all_gather(accumulated_sum, 'wide', axis=0, tiled=True)]
    pallas_call x1 -> x2, Pallas kernels: 12.8 us -> 47.6 us  [the longest x1 34.9 us: placed_blocks(): pl.pallas_call(place_kernel, out_shape=(jax.ShapeDtypeStruct((SLOTS, ROWS...]
    unnamed x1 -> x0, blocking collectives: 13.5 us -> none
    all_to_all x1 -> x0, blocking collectives: 13.4 us -> none  [summed_on_arrival(): lax.all_to_all(pieces, axis, split_axis=0, concat_axis=0, tiled=True)]
    all_to_all x1 -> x0, starting transfers between devices: 13.3 us -> none  [from_everyone(): lax.all_to_all(jnp.broadcast_to(array[None], (devices, *array.shape)), ax...]
    all_to_all x1 -> x0, waiting for transfers between devices: 8.09 us -> none  [from_everyone(): lax.all_to_all(jnp.broadcast_to(array[None], (devices, *array.shape)), ax...]
    dot_general x1 -> x0, matrix products: 6.18 us -> none  [place(): jnp.einsum('sk,kjm->sjm', pick.astype(jnp.float32), blocks_in, precision=...]
    slice x27 -> x0, local copies, waits for them, and re-layouts: 6.07 us -> none  [the longest x26 3.64 us: folded_in_pairs(): part[side::2]]
  transfers between devices with their start and end apart: 2 -> 0, of which waited for: 2 -> 0; matrix products, arithmetic and copies ran while one was open for 7% -> 0% of each run, Pallas kernels for 0% -> 0%
where the time goes in v2:
time: 51.8 us; the launch traced here: 51.6 us
  Pallas kernels  47.6 us (92%)
  local copies, waits for them, and re-layouts  2.74 us (5%)
  between operations  1.29 us (2%)
    pallas_call x1, Pallas kernels, placed_blocks(): pl.pallas_call(place_kernel, out_shape=(jax.ShapeDtypeStruct((SLOTS, ROWS...  34.9 us
    pallas_call x1, Pallas kernels, partial_sums(): pl.pallas_call(partial_kernel, out_shape=jax.ShapeDtypeStruct((SLOTS, BLO...  12.7 us
    unnamed x2, local copies, waits for them, and re-layouts  2.74 us

profile of v2, /device:TPU:1, one launch (start us, length us, event | category | flops | bytes accessed | tf_op | source)
XLA Modules:
  0.0 51.6 jit_solution(16716236891760405477)
XLA Ops:
  1.3 12.7 %partial_sums.1.partial = f32[8,128,128]{2,1,0:T(8,128)} custom-call(s32[192]{0:T(256)} %target.1, s32[1]{0:T(128)S(6)} %copy.10.counts, f32[192,128,128]{2,1,0:T(8,128)} %a_hbm.1, s32[192,128]{1,0:T(8,128)} %row_map.1, s32[192,128]{1,0:T(8,128)} %col_map.1), custom_call_target="tpu_custom_call" | custom-call | tf_op jit(solution)/shard_map/partial_sums/pallas_call | solution.py:76
  14.0 34.9 %placed_blocks.1 = (f32[8,32,128]{2,1,0:T(8,128)}, s32[1,8]{1,0:T(1,128)}) custom-call(s32[1]{0:T(128)S(6)} %copy.10.counts, s32[8]{0:T(128)} %weights.1, f32[8,128,128]{2,1,0:T(8,128)} %partial_sums.1.partial), custom_call_target="tpu_custom_call" | custom-call | tf_op jit(solution)/shard_map/placed_blocks/pallas_call | solution.py:269
  48.9 1.6 %copy.11 = f32[8,32,128]{2,1,0:T(8,128)} copy(f32[8,32,128]{2,1,0:T(8,128)} %get-tuple-element.8) | data formatting | bytes 262144
  50.5 1.2 %copy.12 = s32[8]{0:T(128)} copy(s32[8]{0:T(128)} %bitcast.1) | data formatting | bytes 64

commit v3 on v2

--- a/solution.py
+++ b/solution.py
@@ -8,7 +8,7 @@
 from jax.sharding import PartitionSpec as P
 
 BLOCK = 128
-GROUP = 16
+GROUP = 32
 SLOTS = 8
 WIDE = 64
 NARROW = 4
@@ -17,6 +17,12 @@
 X = CHIPS // Z
 ROWS = BLOCK // NARROW
 HALF = SLOTS // 2
+FINE = 192
+PADDED = 256
+UNIT = 4
+STEP = 6
+RUNS = (FINE + SLOTS * (UNIT - 1)) // UNIT
+VMEM_LIMIT = 48 * 2**20
 F32 = jnp.float32
 I32 = jnp.int32
 BF16 = jnp.bfloat16
@@ -44,54 +50,65 @@
     )
 
 
-def partial_kernel(target, counts, a_hbm, row_map, col_map, out, a_vmem, arrived):
-    steps = a_hbm.shape[0] // GROUP
-
-    def copy(i):
-        part = pl.ds(i * GROUP, GROUP)
-        return pltpu.make_async_copy(a_hbm.at[part], a_vmem.at[part], arrived.at[i])
-
-    for i in range(steps):
-        copy(i).start()
-    out[...] = jnp.zeros_like(out)
-    live = counts[0]
-    sublane = lax.broadcasted_iota(I32, (BLOCK, BLOCK), 0)
-
-    def step(i, carry):
-        copy(i).wait()
-        for j in range(GROUP):
-            b = i * GROUP + j
-            out[lax.rem(target[b], live)] += reduced_block(
-                a_vmem[b], row_map[pl.ds(b, 1), :], col_map[pl.ds(b, 1), :], sublane
-            )
-        return carry
-
-    lax.fori_loop(0, steps, step, 0)
-
-
-def partial_sums(a_blocks, row_map, col_map, target, counts):
-    n = a_blocks.shape[0]
-    smem = pl.BlockSpec(memory_space=pltpu.SMEM)
-    vmem = pl.BlockSpec(memory_space=pltpu.VMEM)
-    return pl.pallas_call(
-        partial_kernel,
-        out_shape=jax.ShapeDtypeStruct((SLOTS, BLOCK, BLOCK), F32),
-        in_specs=[smem, smem, pl.BlockSpec(memory_space=pl.ANY), vmem, vmem],
-        out_specs=vmem,
-        scratch_shapes=[
-            pltpu.VMEM((n, BLOCK, BLOCK), F32),
-            pltpu.SemaphoreType.DMA((n // GROUP,)),
-        ],
-        name="partial_sums",
-    )(target, counts, a_blocks, row_map, col_map)
-
-
-def place_kernel(
-    counts, weights, partial, coarse, offset,
+def order_table(target, live):
+    padded = (PADDED, PADDED)
+    one, zero = jnp.ones(padded, F32), jnp.zeros(padded, F32)
+    code = target.astype(F32)
+    count = jnp.full((1, FINE), jnp.maximum(live, 1), I32).astype(F32)
+    slot = code - jnp.floor((code + 0.5) / count) * count
+    slot = jnp.concatenate([slot, jnp.full((1, PADDED - FINE), SLOTS, F32)], 1)
+    lane = lax.broadcasted_iota(I32, padded, 1)
+    sublane = lax.broadcasted_iota(I32, padded, 0)
+    across = jnp.broadcast_to(slot, padded)
+    down = jnp.sum(jnp.where(lane == sublane, across, zero), 1, keepdims=True)
+    place = jnp.sum(jnp.where((across == down) & (lane < sublane), one, zero), 1, keepdims=True)
+    place = jnp.where(down == SLOTS, F32(1e6), place)
+    column = lax.broadcasted_iota(I32, (1, PADDED), 1)
+    base = jnp.zeros((1, 1), F32)
+    keep = jnp.ones((1, PADDED), F32)
+    last = jnp.zeros((1, PADDED), F32)
+    for s in range(SLOTS):
+        size = jnp.sum(jnp.where(slot == s, F32(1), F32(0)), 1, keepdims=True)
+        runs = jnp.floor((size + (UNIT - 1)) * (1.0 / UNIT))
+        place = place + jnp.where(down == s, base * UNIT, F32(0))
+        keep = jnp.where((column.astype(F32) == base) & (size > 0), F32(0), keep)
+        last = jnp.where(column == s, jnp.where(size > 0, base + runs - 1, F32(RUNS)), last)
+        base = base + runs
+    found = jnp.where(place == lane.astype(F32), sublane.astype(F32) + 1, zero)
+    found = jnp.sum(found, 0, keepdims=True)
+    source = jnp.where(found > 0, found - 1, F32(FINE))
+    return jnp.concatenate([source, keep, last, jnp.zeros((5, PADDED), F32)], 0).astype(I32)
+
+
+def coarse_kernel(
+    counts, weights_hbm, target_hbm, row_hbm, col_hbm, a_hbm, back, note_out,
+    weights, target, a_vmem, row_map, col_map, reduced, run_sums, table, order, partial,
     meta_own, meta, via_up, via_down, send_up, send_down, from_down, from_up,
-    rows_out, rows_in, pick, placed, back, note_own, note_in,
+    rows_out, rows_in, pick, placed, note_own, note_in,
+    a_got, map_got, order_got,
     y_sent, y_got, meta_sent, meta_got, out_sent, out_got, back_sent, back_got, note_sent, note_got,
 ):
+    steps = FINE // GROUP
+
+    def a_copy(i):
+        part = pl.ds(i * GROUP, GROUP)
+        return pltpu.make_async_copy(a_hbm.at[part], a_vmem.at[part], a_got.at[i])
+
+    row_copy = pltpu.make_async_copy(row_hbm, row_map, map_got.at[0])
+    col_copy = pltpu.make_async_copy(col_hbm, col_map, map_got.at[1])
+    small_copies = [
+        pltpu.make_async_copy(src, dst, map_got.at[2 + k])
+        for k, (src, dst) in enumerate(
+            ((target_hbm, target), (weights_hbm, weights))
+        )
+    ]
+    for copy in small_copies:
+        copy.start()
+    row_copy.start()
+    col_copy.start()
+    for i in range(steps):
+        a_copy(i).start()
+
     w = lax.axis_index("wide")
     y = lax.axis_index("narrow")
     core = lax.rem(w, 2)
@@ -120,6 +137,8 @@
 
     lax.fori_loop(1, WIDE, greet, 0)
 
+    for copy in small_copies:
+        copy.wait()
     lane = lax.broadcasted_iota(I32, (1, BLOCK), 1)
     turn = lax.rem(lane, SLOTS)
     weight_row = jnp.zeros((1, BLOCK), I32)
@@ -127,7 +146,6 @@
         weight_row = jnp.where(turn == s, weights[s], weight_row)
     meta_own[:, :BLOCK] = jnp.full((1, BLOCK), counts[0], I32)
     meta_own[:, BLOCK:] = weight_row
-    pl.semaphore_wait(barrier, WIDE + 1)
 
     def piece(half, owner):
         return partial.at[pl.ds(half * HALF, HALF), pl.ds(owner * ROWS, ROWS), :]
@@ -143,25 +161,67 @@
         )[k]
         return remote(src, dst, y_sent.at[k], y_got.at[k], w, narrow)
 
+    near = [lax.rem(z + Z // 2 + k, Z) for k in range(Z)]
+
+    def each_chip(body):
+        def visit(d, carry):
+            base = lax.rem(x + X // 2 + d, X) * Z
+            for k in range(Z):
+                body(base + near[k])
+            return carry
+
+        lax.fori_loop(0, X, visit, 0)
+
+    def to_rows(send):
+        def body(there):
+            @pl.when((there != chip) | (core == 0))
+            def _():
+                send(there).start()
+
+        each_chip(body)
+
+    table[...] = order_table(target[...], counts[0])
+    order_copy = pltpu.make_async_copy(table, order, order_got)
+    order_copy.start()
+    reduced[FINE] = jnp.zeros((BLOCK, BLOCK), F32)
+    run_sums[RUNS] = jnp.zeros((BLOCK, BLOCK), F32)
+    sublane = lax.broadcasted_iota(I32, (BLOCK, BLOCK), 0)
+
+    def reduce_group(i, carry):
+        @pl.when(i == steps - 2)
+        def _():
+            pl.semaphore_wait(barrier, WIDE + 1)
+            to_rows(lambda there: remote(
+                meta_own, meta.at[w], meta_sent, meta_got, 2 * there + 1, y))
+
+        a_copy(i).wait()
+        for j in range(GROUP):
+            b = i * GROUP + j
+            reduced[b] = reduced_block(
+                a_vmem[b], row_map[pl.ds(b, 1), :], col_map[pl.ds(b, 1), :], sublane
+            )
+        return carry
+
+    row_copy.wait()
+    col_copy.wait()
+    lax.fori_loop(0, steps, reduce_group, 0)
+    order_copy.wait()
+
+    def add_runs(i, total):
+        for k in range(STEP):
+            run = i * STEP + k
+            total = total * order[1, run].astype(F32)
+            for u in range(UNIT):
+                total = total + reduced[jnp.clip(order[0, run * UNIT + u], 0, FINE)]
+            run_sums[run] = total
+        return total
+
+    lax.fori_loop(0, RUNS // STEP, add_runs, jnp.zeros((BLOCK, BLOCK), F32))
+    for s in range(SLOTS):
+        partial[s] = run_sums[jnp.clip(order[2, s], 0, RUNS)]
+
     for k in range(4):
         y_copy(k).start()
-
-    def each_chip(body):
-        def visit(d, carry):
-            dx = lax.rem(X // 2 + lax.div(d, Z), X)
-            dz = lax.rem(Z // 2 + lax.rem(d, Z), Z)
-            there = lax.rem(x + dx, X) * Z + lax.rem(z + dz, Z)
-
-            @pl.when((there != chip) | (core == 0))
-            def _():
-                body(there)
-
-            return carry
-
-        lax.fori_loop(0, CHIPS, visit, 0)
-
-    each_chip(lambda there: remote(
-        meta_own, meta.at[w], meta_sent, meta_got, 2 * there + 1, y).start())
 
     y_copy(0).wait_recv()
     send_up[...] = via_up[...] + partial[pl.ds(0, HALF), pl.ds(up * ROWS, ROWS), :]
@@ -200,7 +260,7 @@
             if k == 0:
                 note_own[...] = line
             else:
-                offset[...] = line[:, :SLOTS]
+                note_out[...] = line
         note = remote(note_own, note_in, note_sent, note_got, w - 1, y)
         note.start()
 
@@ -211,8 +271,8 @@
             partial[s, pl.ds(y * ROWS, ROWS), :] + from_down[s] + from_up[s]
         )
 
-    each_chip(lambda there: remote(
-        rows_out.at[there], rows_in.at[w], out_sent, out_got, 2 * there + 1, y).start())
+    to_rows(lambda there: remote(
+        rows_out.at[there], rows_in.at[w], out_sent, out_got, 2 * there + 1, y))
 
     @pl.when(core == 1)
     def _():
@@ -224,12 +284,14 @@
         placed[...] = (both[:, :BLOCK] + both[:, BLOCK:]).reshape(WIDE, SLOTS, BLOCK)
         back[chip] = placed[w]
 
-        def deliver(d, carry):
-            there = lax.rem(w + d, WIDE)
-            remote(placed.at[there], back.at[chip], back_sent, back_got, there, y).start()
-            return carry
-
-        lax.fori_loop(1, WIDE, deliver, 0)
+        def deliver(there):
+            remote(placed.at[2 * there], back.at[chip], back_sent, back_got, 2 * there, y).start()
+
+            @pl.when(there != chip)
+            def _():
+                remote(placed.at[2 * there + 1], back.at[chip], back_sent, back_got, 2 * there + 1, y).start()
+
+        each_chip(deliver)
         few = back.at[pl.ds(0, CHIPS - 1)]
         remote(few, few, back_sent, back_got, w - 1, y).wait_recv()
 
@@ -237,10 +299,7 @@
     def _():
         remote(back, back, back_sent, back_got, w + 1, y).wait_recv()
         remote(note_in, note_in, note_sent, note_got, w + 1, y).wait_recv()
-        offset[...] = note_in[:, :SLOTS]
-
-    for s in range(SLOTS):
-        coarse[s] = back[:, s, :]
+        note_out[...] = note_in[...]
 
     for k in range(6):
         y_copy(k).wait_send()
@@ -262,45 +321,68 @@
         remote(some, some, meta_sent, meta_got, w + 1, y).wait_send()
 
 
-def placed_blocks(counts, weights, partial):
-    smem = pl.BlockSpec(memory_space=pltpu.SMEM)
+def finish_kernel(back, note, coarse, offset):
+    for s in range(SLOTS):
+        coarse[s] = back[:, s, :]
+    offset[...] = note[:, :SLOTS]
+
+
+def local(a_blocks, row_map, col_map, target, counts, weights):
     vmem = pl.BlockSpec(memory_space=pltpu.VMEM)
+    hbm = pl.BlockSpec(memory_space=pltpu.HBM)
     dma = pltpu.SemaphoreType.DMA
-    return pl.pallas_call(
-        place_kernel,
+    half = pltpu.VMEM((HALF, ROWS, BLOCK), F32)
+    full = pltpu.VMEM((SLOTS, ROWS, BLOCK), F32)
+    plane = pltpu.VMEM((WIDE, SLOTS, BLOCK), F32)
+    line = pltpu.VMEM((1, BLOCK), I32)
+    back, note = pl.pallas_call(
+        coarse_kernel,
+        out_shape=(
+            jax.ShapeDtypeStruct((CHIPS, SLOTS, BLOCK), F32),
+            jax.ShapeDtypeStruct((1, BLOCK), I32),
+        ),
+        in_specs=[pl.BlockSpec(memory_space=pltpu.SMEM)] + [hbm] * 5,
+        out_specs=(vmem, vmem),
+        scratch_shapes=[
+            pltpu.SMEM((SLOTS,), I32),
+            pltpu.VMEM((1, FINE), I32),
+            pltpu.VMEM((FINE, BLOCK, BLOCK), F32),
+            pltpu.VMEM((FINE, BLOCK), I32),
+            pltpu.VMEM((FINE, BLOCK), I32),
+            pltpu.VMEM((FINE + 1, BLOCK, BLOCK), F32),
+            pltpu.VMEM((RUNS + 1, BLOCK, BLOCK), F32),
+            pltpu.VMEM((8, PADDED), I32),
+            pltpu.SMEM((8, PADDED), I32),
+            pltpu.VMEM((SLOTS, BLOCK, BLOCK), F32),
+            pltpu.VMEM((1, 2 * BLOCK), I32),
+            pltpu.VMEM((WIDE, 1, 2 * BLOCK), I32),
+            half, half, half, half, full, full,
+            pltpu.VMEM((CHIPS, SLOTS, BLOCK), F32),
+            plane,
+            pltpu.VMEM((WIDE * SLOTS, WIDE * SLOTS), BF16),
+            plane,
+            line, line,
+            dma((FINE // GROUP,)), dma((4,)), dma,
+            dma((6,)), dma((6,)),
+            dma, dma, dma, dma, dma, dma, dma, dma,
+        ],
+        compiler_params=pltpu.CompilerParams(
+            collective_id=0, has_side_effects=True, vmem_limit_bytes=VMEM_LIMIT
+        ),
+        name="coarse_blocks",
+    )(counts, *(pltpu.with_memory_space_constraint(each, pltpu.HBM) for each in (
+        weights, target.reshape(1, FINE), row_map, col_map, a_blocks)))
+    coarse, offset = pl.pallas_call(
+        finish_kernel,
         out_shape=(
             jax.ShapeDtypeStruct((SLOTS, ROWS, BLOCK), F32),
             jax.ShapeDtypeStruct((1, SLOTS), I32),
         ),
-        in_specs=[smem, smem, vmem],
+        in_specs=[vmem, vmem],
         out_specs=(vmem, vmem),
-        scratch_shapes=[
-            pltpu.VMEM((1, 2 * BLOCK), I32),
-            pltpu.VMEM((WIDE, 1, 2 * BLOCK), I32),
-            pltpu.VMEM((HALF, ROWS, BLOCK), F32),
-            pltpu.VMEM((HALF, ROWS, BLOCK), F32),
-            pltpu.VMEM((HALF, ROWS, BLOCK), F32),
-            pltpu.VMEM((HALF, ROWS, BLOCK), F32),
-            pltpu.VMEM((SLOTS, ROWS, BLOCK), F32),
-            pltpu.VMEM((SLOTS, ROWS, BLOCK), F32),
-            pltpu.VMEM((CHIPS, SLOTS, BLOCK), F32),
-            pltpu.VMEM((WIDE, SLOTS, BLOCK), F32),
-            pltpu.VMEM((WIDE * SLOTS, WIDE * SLOTS), BF16),
-            pltpu.VMEM((WIDE, SLOTS, BLOCK), F32),
-            pltpu.VMEM((CHIPS, SLOTS, BLOCK), F32),
-            pltpu.VMEM((1, BLOCK), I32),
-            pltpu.VMEM((1, BLOCK), I32),
-            dma((6,)), dma((6,)),
-            dma, dma, dma, dma, dma, dma, dma, dma,
-        ],
-        compiler_params=pltpu.CompilerParams(collective_id=0, has_side_effects=True),
-        name="placed_blocks",
-    )(counts, weights, partial)
-
-
-def local(a_blocks, row_map, col_map, target, counts, weights):
-    partial = partial_sums(a_blocks, row_map, col_map, target, counts)
-    coarse, offset = placed_blocks(counts, weights, partial)
+        compiler_params=pltpu.CompilerParams(vmem_limit_bytes=4 * 2**20),
+        name="finish",
+    )(back, note)
     return coarse, offset.reshape(SLOTS)
 
 

time: 51.8 us -> 43.3 us (0.84)
  Pallas kernels: 47.6 us -> 42 us
  local copies, waits for them, and re-layouts: 2.74 us -> 0 us
    pallas_call x2, Pallas kernels: 47.6 us -> 42 us  [the longest x1 41.2 us: local(): pl.pallas_call(coarse_kernel, out_shape=(jax.ShapeDtypeStruct((CHIPS, SLO...]
    unnamed x2 -> x0, local copies, waits for them, and re-layouts: 2.74 us -> none
where the time goes in v3:
time: 43.3 us
  Pallas kernels  42 us (97%)
  between operations  1.29 us (3%)
    pallas_call x1, Pallas kernels, local(): pl.pallas_call(coarse_kernel, out_shape=(jax.ShapeDtypeStruct((CHIPS, SLO...  41.2 us

profile of v3, /device:TPU:1, one launch (start us, length us, event | category | flops | bytes accessed | tf_op | source)
XLA Modules:
  0.0 43.3 jit_solution(5762361950265599913)
XLA Ops:
  1.3 41.2 %coarse_blocks.1 = (f32[32,8,128]{2,1,0:T(8,128)S(1)}, s32[1,128]{1,0:T(1,128)S(1)}) custom-call(s32[1]{0:T(128)S(6)} %copy.8.counts, s32[8]{0:T(128)} %weights_hbm.1, s32[1,192]{1,0:T(1,128)} %bitcast.2, s32[192,128]{1,0:T(8,128)} %row_hbm.1, s32[192,128]{1,0:T(8,128)} %col_hbm.1, f32[192,128,128]{2,1,0:T(8,128)} %a_hbm.1), custom_call_target="tpu_custom_call" | custom-call | tf_op jit(solution)/shard_map/coarse_blocks/pallas_call | solution.py:338
  42.5 0.7 %finish.1 = (f32[8,32,128]{2,1,0:T(8,128)}, s32[1,8]{1,0:T(1,128)}) custom-call(f32[32,8,128]{2,1,0:T(8,128)S(1)} %get-tuple-element.6.back, s32[1,128]{1,0:T(1,128)S(1)} %get-tuple-element.7.note), custom_call_target="tpu_custom_call" | custom-call | tf_op jit(solution)/shard_map/finish/pallas_call | solution.py:375

commit v4 on v3

--- a/solution.py
+++ b/solution.py
@@ -20,7 +20,7 @@
 FINE = 192
 PADDED = 256
 UNIT = 4
-STEP = 6
+STEP = 18
 RUNS = (FINE + SLOTS * (UNIT - 1)) // UNIT
 VMEM_LIMIT = 48 * 2**20
 F32 = jnp.float32
@@ -33,21 +33,19 @@
     return high, (value - high.astype(F32)).astype(BF16)
 
 
-def reduced_block(a, row, col, sublane):
-    one, zero = F32(1), F32(0)
-    pick_row = jnp.where(sublane == row, one, zero).astype(BF16)
-    pick_col = jnp.where(sublane == col, one, zero).astype(BF16)
-    merged = jnp.dot(
-        jnp.concatenate([pick_row, pick_row], 1),
-        jnp.concatenate(split(a), 0),
-        preferred_element_type=F32,
-    )
-    return lax.dot_general(
-        jnp.concatenate(split(merged), 1),
-        jnp.concatenate([pick_col, pick_col], 1),
+def merged_block(a, col, sublane):
+    chosen = picked(col, sublane)
+    merged = lax.dot_general(
+        jnp.concatenate(split(a), 1),
+        jnp.concatenate([chosen, chosen], 1),
         (((1,), (1,)), ((), ())),
         preferred_element_type=F32,
     )
+    return jnp.concatenate(split(merged), 1)
+
+
+def picked(index, sublane):
+    return jnp.where(sublane == index, F32(1), F32(0)).astype(BF16)
 
 
 def order_table(target, live):
@@ -82,7 +80,7 @@
 
 def coarse_kernel(
     counts, weights_hbm, target_hbm, row_hbm, col_hbm, a_hbm, back, note_out,
-    weights, target, a_vmem, row_map, col_map, reduced, run_sums, table, order, partial,
+    weights, target, a_vmem, row_map, col_map, merged, run_sums, table, order, partial,
     meta_own, meta, via_up, via_down, send_up, send_down, from_down, from_up,
     rows_out, rows_in, pick, placed, note_own, note_in,
     a_got, map_got, order_got,
@@ -94,7 +92,7 @@
         part = pl.ds(i * GROUP, GROUP)
         return pltpu.make_async_copy(a_hbm.at[part], a_vmem.at[part], a_got.at[i])
 
-    row_copy = pltpu.make_async_copy(row_hbm, row_map, map_got.at[0])
+    row_copy = pltpu.make_async_copy(row_hbm, row_map.at[pl.ds(0, FINE)], map_got.at[0])
     col_copy = pltpu.make_async_copy(col_hbm, col_map, map_got.at[1])
     small_copies = [
         pltpu.make_async_copy(src, dst, map_got.at[2 + k])
@@ -183,7 +181,8 @@
     table[...] = order_table(target[...], counts[0])
     order_copy = pltpu.make_async_copy(table, order, order_got)
     order_copy.start()
-    reduced[FINE] = jnp.zeros((BLOCK, BLOCK), F32)
+    merged[FINE] = jnp.zeros((BLOCK, 2 * BLOCK), BF16)
+    row_map[pl.ds(FINE, SLOTS), :] = jnp.zeros((SLOTS, BLOCK), I32)
     run_sums[RUNS] = jnp.zeros((BLOCK, BLOCK), F32)
     sublane = lax.broadcasted_iota(I32, (BLOCK, BLOCK), 0)
 
@@ -197,22 +196,25 @@
         a_copy(i).wait()
         for j in range(GROUP):
             b = i * GROUP + j
-            reduced[b] = reduced_block(
-                a_vmem[b], row_map[pl.ds(b, 1), :], col_map[pl.ds(b, 1), :], sublane
-            )
+            merged[b] = merged_block(a_vmem[b], col_map[pl.ds(b, 1), :], sublane)
         return carry
 
-    row_copy.wait()
     col_copy.wait()
     lax.fori_loop(0, steps, reduce_group, 0)
+    row_copy.wait()
     order_copy.wait()
 
     def add_runs(i, total):
         for k in range(STEP):
             run = i * STEP + k
-            total = total * order[1, run].astype(F32)
-            for u in range(UNIT):
-                total = total + reduced[jnp.clip(order[0, run * UNIT + u], 0, FINE)]
+            at = [jnp.clip(order[0, run * UNIT + u], 0, FINE) for u in range(UNIT)]
+            added = jnp.dot(
+                jnp.concatenate([picked(row_map[pl.ds(b, 1), :], sublane) for b in at], 1),
+                jnp.concatenate([merged[b] for b in at], 0),
+                preferred_element_type=F32,
+            )
+            added = added[:, :BLOCK] + added[:, BLOCK:]
+            total = total * order[1, run].astype(F32) + added
             run_sums[run] = total
         return total
 
@@ -347,9 +349,9 @@
             pltpu.SMEM((SLOTS,), I32),
             pltpu.VMEM((1, FINE), I32),
             pltpu.VMEM((FINE, BLOCK, BLOCK), F32),
+            pltpu.VMEM((FINE + SLOTS, BLOCK), I32),
             pltpu.VMEM((FINE, BLOCK), I32),
-            pltpu.VMEM((FINE, BLOCK), I32),
-            pltpu.VMEM((FINE + 1, BLOCK, BLOCK), F32),
+            pltpu.VMEM((FINE + 1, BLOCK, 2 * BLOCK), BF16),
             pltpu.VMEM((RUNS + 1, BLOCK, BLOCK), F32),
             pltpu.VMEM((8, PADDED), I32),
             pltpu.SMEM((8, PADDED), I32),

time: 43.3 us -> 41.1 us (0.949)
  Pallas kernels: 42 us -> 39.7 us
    pallas_call x1, Pallas kernels: 41.2 us -> 39 us  [local(): pl.pallas_call(coarse_kernel, out_shape=(jax.ShapeDtypeStruct((CHIPS, SLO...]
where the time goes in v4:
time: 41.1 us; the launch traced here: 41 us
  Pallas kernels  39.7 us (97%)
  between operations  1.29 us (3%)
    pallas_call x1, Pallas kernels, local(): pl.pallas_call(coarse_kernel, out_shape=(jax.ShapeDtypeStruct((CHIPS, SLO...  39 us

profile of v4, /device:TPU:1, one launch (start us, length us, event | category | flops | bytes accessed | tf_op | source)
XLA Modules:
  0.0 41.0 jit_solution(7927540071047952783)
XLA Ops:
  1.3 39.0 %coarse_blocks.1 = (f32[32,8,128]{2,1,0:T(8,128)S(1)}, s32[1,128]{1,0:T(1,128)S(1)}) custom-call(s32[1]{0:T(128)S(6)} %copy.8.counts, s32[8]{0:T(128)} %weights_hbm.1, s32[1,192]{1,0:T(1,128)} %bitcast.2, s32[192,128]{1,0:T(8,128)} %row_hbm.1, s32[192,128]{1,0:T(8,128)} %col_hbm.1, f32[192,128,128]{2,1,0:T(8,128)} %a_hbm.1), custom_call_target="tpu_custom_call" | custom-call | tf_op jit(solution)/shard_map/coarse_blocks/pallas_call | solution.py:340
  40.3 0.7 %finish.1 = (f32[8,32,128]{2,1,0:T(8,128)}, s32[1,8]{1,0:T(1,128)}) custom-call(f32[32,8,128]{2,1,0:T(8,128)S(1)} %get-tuple-element.6.back, s32[1,128]{1,0:T(1,128)S(1)} %get-tuple-element.7.note), custom_call_target="tpu_custom_call" | custom-call | tf_op jit(solution)/shard_map/finish/pallas_call | solution.py:377

commit v5 on v4

--- a/solution.py
+++ b/solution.py
@@ -8,7 +8,7 @@
 from jax.sharding import PartitionSpec as P
 
 BLOCK = 128
-GROUP = 32
+GROUP = 24
 SLOTS = 8
 WIDE = 64
 NARROW = 4
@@ -20,7 +20,8 @@
 FINE = 192
 PADDED = 256
 UNIT = 4
-STEP = 18
+STEP = 27
+AHEAD = 3
 RUNS = (FINE + SLOTS * (UNIT - 1)) // UNIT
 VMEM_LIMIT = 48 * 2**20
 F32 = jnp.float32
@@ -100,12 +101,10 @@
             ((target_hbm, target), (weights_hbm, weights))
         )
     ]
+    a_copy(0).start()
     for copy in small_copies:
         copy.start()
-    row_copy.start()
     col_copy.start()
-    for i in range(steps):
-        a_copy(i).start()
 
     w = lax.axis_index("wide")
     y = lax.axis_index("narrow")
@@ -127,23 +126,6 @@
     for other in (up, down):
         pl.semaphore_signal(barrier, inc=1, device_id={"wide": w, "narrow": other},
                             device_id_type=pl.DeviceIdType.MESH)
-
-    def greet(d, carry):
-        pl.semaphore_signal(barrier, inc=1, device_id={"wide": lax.rem(w + d, WIDE), "narrow": y},
-                            device_id_type=pl.DeviceIdType.MESH)
-        return carry
-
-    lax.fori_loop(1, WIDE, greet, 0)
-
-    for copy in small_copies:
-        copy.wait()
-    lane = lax.broadcasted_iota(I32, (1, BLOCK), 1)
-    turn = lax.rem(lane, SLOTS)
-    weight_row = jnp.zeros((1, BLOCK), I32)
-    for s in range(SLOTS):
-        weight_row = jnp.where(turn == s, weights[s], weight_row)
-    meta_own[:, :BLOCK] = jnp.full((1, BLOCK), counts[0], I32)
-    meta_own[:, BLOCK:] = weight_row
 
     def piece(half, owner):
         return partial.at[pl.ds(half * HALF, HALF), pl.ds(owner * ROWS, ROWS), :]
@@ -178,6 +160,29 @@
 
         each_chip(body)
 
+    def greet(there):
+        pl.semaphore_signal(barrier, inc=1, device_id={"wide": 2 * there + 1 - core, "narrow": y},
+                            device_id_type=pl.DeviceIdType.MESH)
+
+        @pl.when(there != chip)
+        def _():
+            pl.semaphore_signal(barrier, inc=1, device_id={"wide": 2 * there + core, "narrow": y},
+                                device_id_type=pl.DeviceIdType.MESH)
+
+    each_chip(greet)
+    row_copy.start()
+    for i in range(1, AHEAD):
+        a_copy(i).start()
+    for copy in small_copies:
+        copy.wait()
+    lane = lax.broadcasted_iota(I32, (1, BLOCK), 1)
+    turn = lax.rem(lane, SLOTS)
+    weight_row = jnp.zeros((1, BLOCK), I32)
+    for s in range(SLOTS):
+        weight_row = jnp.where(turn == s, weights[s], weight_row)
+    meta_own[:, :BLOCK] = jnp.full((1, BLOCK), counts[0], I32)
+    meta_own[:, BLOCK:] = weight_row
+
     table[...] = order_table(target[...], counts[0])
     order_copy = pltpu.make_async_copy(table, order, order_got)
     order_copy.start()
@@ -187,13 +192,12 @@
     sublane = lax.broadcasted_iota(I32, (BLOCK, BLOCK), 0)
 
     def reduce_group(i, carry):
-        @pl.when(i == steps - 2)
+        a_copy(i).wait()
+
+        @pl.when(i + AHEAD < steps)
         def _():
-            pl.semaphore_wait(barrier, WIDE + 1)
-            to_rows(lambda there: remote(
-                meta_own, meta.at[w], meta_sent, meta_got, 2 * there + 1, y))
-
-        a_copy(i).wait()
+            a_copy(i + AHEAD).start()
+
         for j in range(GROUP):
             b = i * GROUP + j
             merged[b] = merged_block(a_vmem[b], col_map[pl.ds(b, 1), :], sublane)
@@ -222,8 +226,11 @@
     for s in range(SLOTS):
         partial[s] = run_sums[jnp.clip(order[2, s], 0, RUNS)]
 
+    pl.semaphore_wait(barrier, WIDE + 1)
     for k in range(4):
         y_copy(k).start()
+    to_rows(lambda there: remote(
+        meta_own, meta.at[w], meta_sent, meta_got, 2 * there + 1, y))
 
     y_copy(0).wait_recv()
     send_up[...] = via_up[...] + partial[pl.ds(0, HALF), pl.ds(up * ROWS, ROWS), :]
@@ -232,8 +239,19 @@
     send_down[...] = via_down[...] + partial[pl.ds(HALF, HALF), pl.ds(down * ROWS, ROWS), :]
     y_copy(5).start()
 
+    for k in (2, 3, 4, 5):
+        y_copy(k).wait_recv()
+    for s in range(SLOTS):
+        rows_out[:, s, :] = (
+            partial[s, pl.ds(y * ROWS, ROWS), :] + from_down[s] + from_up[s]
+        )
+
+    to_rows(lambda there: remote(
+        rows_out.at[there], rows_in.at[w], out_sent, out_got, 2 * there + 1, y))
+
     @pl.when(core == 1)
     def _():
+        rows_in[w] = rows_out[chip]
         meta[w] = meta_own[...]
         remote(meta.at[pl.ds(0, WIDE - 1)], meta.at[pl.ds(0, WIDE - 1)], meta_sent, meta_got, w - 1, y).wait_recv()
         total = WIDE * SLOTS
@@ -265,20 +283,6 @@
                 note_out[...] = line
         note = remote(note_own, note_in, note_sent, note_got, w - 1, y)
         note.start()
-
-    for k in (2, 3, 4, 5):
-        y_copy(k).wait_recv()
-    for s in range(SLOTS):
-        rows_out[:, s, :] = (
-            partial[s, pl.ds(y * ROWS, ROWS), :] + from_down[s] + from_up[s]
-        )
-
-    to_rows(lambda there: remote(
-        rows_out.at[there], rows_in.at[w], out_sent, out_got, 2 * there + 1, y))
-
-    @pl.when(core == 1)
-    def _():
-        rows_in[w] = rows_out[chip]
         most = rows_in.at[pl.ds(0, WIDE - 1)]
         remote(most, most, out_sent, out_got, w - 1, y).wait_recv()
         high, low = split(rows_in[...].reshape(WIDE * SLOTS, BLOCK))

time: 41.1 us -> 38.7 us (0.942)
  Pallas kernels: 39.7 us -> 37.3 us
    pallas_call x1, Pallas kernels: 39 us -> 36.5 us  [local(): pl.pallas_call(coarse_kernel, out_shape=(jax.ShapeDtypeStruct((CHIPS, SLO...]
where the time goes in v5:
time: 38.7 us; the launch traced here: 38.6 us
  Pallas kernels  37.3 us (96%)
  between operations  1.29 us (3%)
    pallas_call x1, Pallas kernels, local(): pl.pallas_call(coarse_kernel, out_shape=(jax.ShapeDtypeStruct((CHIPS, SLO...  36.5 us

profile of v5, /device:TPU:1, one launch (start us, length us, event | category | flops | bytes accessed | tf_op | source)
XLA Modules:
  0.0 38.6 jit_solution(9407315796928677713)
XLA Ops:
  1.3 36.5 %coarse_blocks.1 = (f32[32,8,128]{2,1,0:T(8,128)S(1)}, s32[1,128]{1,0:T(1,128)S(1)}) custom-call(s32[1]{0:T(128)S(6)} %copy.8.counts, s32[8]{0:T(128)} %weights_hbm.1, s32[1,192]{1,0:T(1,128)} %bitcast.2, s32[192,128]{1,0:T(8,128)} %row_hbm.1, s32[192,128]{1,0:T(8,128)} %col_hbm.1, f32[192,128,128]{2,1,0:T(8,128)} %a_hbm.1), custom_call_target="tpu_custom_call" | custom-call | tf_op jit(solution)/shard_map/coarse_blocks/pallas_call | solution.py:344
  37.8 0.7 %finish.1 = (f32[8,32,128]{2,1,0:T(8,128)}, s32[1,8]{1,0:T(1,128)}) custom-call(f32[32,8,128]{2,1,0:T(8,128)S(1)} %get-tuple-element.6.back, s32[1,128]{1,0:T(1,128)S(1)} %get-tuple-element.7.note), custom_call_target="tpu_custom_call" | custom-call | tf_op jit(solution)/shard_map/finish/pallas_call | solution.py:381

commit v6 on v5

--- a/solution.py
+++ b/solution.py
@@ -127,18 +127,25 @@
         pl.semaphore_signal(barrier, inc=1, device_id={"wide": w, "narrow": other},
                             device_id_type=pl.DeviceIdType.MESH)
 
-    def piece(half, owner):
-        return partial.at[pl.ds(half * HALF, HALF), pl.ds(owner * ROWS, ROWS), :]
+    def piece(slot, size, owner):
+        return partial.at[pl.ds(slot, size), pl.ds(owner * ROWS, ROWS), :]
 
     def y_copy(k):
-        src, dst, narrow = (
-            (piece(0, far), via_up, up),
-            (piece(1, far), via_down, down),
-            (piece(1, up), from_down.at[pl.ds(HALF, HALF)], up),
-            (piece(0, down), from_up.at[pl.ds(0, HALF)], down),
-            (send_up, from_down.at[pl.ds(0, HALF)], up),
-            (send_down, from_up.at[pl.ds(HALF, HALF)], down),
-        )[k]
+        s = k // 4
+        one = pl.ds(s, 1)
+        other = pl.ds(HALF + s, 1)
+        if k >= 4 * HALF:
+            src, dst, narrow = (
+                (piece(HALF, HALF, up), from_down.at[pl.ds(HALF, HALF)], up),
+                (piece(0, HALF, down), from_up.at[pl.ds(0, HALF)], down),
+            )[k - 4 * HALF]
+        else:
+            src, dst, narrow = (
+                (piece(s, 1, far), via_up.at[one], up),
+                (piece(HALF + s, 1, far), via_down.at[one], down),
+                (send_up.at[one], from_down.at[one], up),
+                (send_down.at[one], from_up.at[other], down),
+            )[k % 4]
         return remote(src, dst, y_sent.at[k], y_got.at[k], w, narrow)
 
     near = [lax.rem(z + Z // 2 + k, Z) for k in range(Z)]
@@ -227,20 +234,25 @@
         partial[s] = run_sums[jnp.clip(order[2, s], 0, RUNS)]
 
     pl.semaphore_wait(barrier, WIDE + 1)
-    for k in range(4):
-        y_copy(k).start()
+    for s in range(HALF):
+        y_copy(4 * s).start()
+        y_copy(4 * s + 1).start()
+    y_copy(4 * HALF).start()
+    y_copy(4 * HALF + 1).start()
     to_rows(lambda there: remote(
         meta_own, meta.at[w], meta_sent, meta_got, 2 * there + 1, y))
 
-    y_copy(0).wait_recv()
-    send_up[...] = via_up[...] + partial[pl.ds(0, HALF), pl.ds(up * ROWS, ROWS), :]
-    y_copy(4).start()
-    y_copy(1).wait_recv()
-    send_down[...] = via_down[...] + partial[pl.ds(HALF, HALF), pl.ds(down * ROWS, ROWS), :]
-    y_copy(5).start()
-
-    for k in (2, 3, 4, 5):
-        y_copy(k).wait_recv()
+    for s in range(HALF):
+        y_copy(4 * s).wait_recv()
+        send_up[s] = via_up[s] + partial[s, pl.ds(up * ROWS, ROWS), :]
+        y_copy(4 * s + 2).start()
+        y_copy(4 * s + 1).wait_recv()
+        send_down[s] = via_down[s] + partial[HALF + s, pl.ds(down * ROWS, ROWS), :]
+        y_copy(4 * s + 3).start()
+
+    for k in range(4 * HALF + 2):
+        if k >= 4 * HALF or k % 4 > 1:
+            y_copy(k).wait_recv()
     for s in range(SLOTS):
         rows_out[:, s, :] = (
             partial[s, pl.ds(y * ROWS, ROWS), :] + from_down[s] + from_up[s]
@@ -307,7 +319,7 @@
         remote(note_in, note_in, note_sent, note_got, w + 1, y).wait_recv()
         note_out[...] = note_in[...]
 
-    for k in range(6):
+    for k in range(4 * HALF + 2):
         y_copy(k).wait_send()
 
     @pl.when(core == 1)
@@ -369,7 +381,7 @@
             plane,
             line, line,
             dma((FINE // GROUP,)), dma((4,)), dma,
-            dma((6,)), dma((6,)),
+            dma((4 * HALF + 2,)), dma((4 * HALF + 2,)),
             dma, dma, dma, dma, dma, dma, dma, dma,
         ],
         compiler_params=pltpu.CompilerParams(

time: 38.7 us -> 38.4 us (level)
  no operation moved by 1% of the time
where the time goes in v6:
time: 38.4 us; the launch traced here: 38.3 us
  Pallas kernels  37 us (96%)
  between operations  1.29 us (3%)
    pallas_call x1, Pallas kernels, local(): pl.pallas_call(coarse_kernel, out_shape=(jax.ShapeDtypeStruct((CHIPS, SLO...  36.3 us

profile of v6, /device:TPU:1, one launch (start us, length us, event | category | flops | bytes accessed | tf_op | source)
XLA Modules:
  0.0 38.3 jit_solution(6474001208398491196)
XLA Ops:
  1.3 36.3 %coarse_blocks.1 = (f32[32,8,128]{2,1,0:T(8,128)S(1)}, s32[1,128]{1,0:T(1,128)S(1)}) custom-call(s32[1]{0:T(128)S(6)} %copy.8.counts, s32[8]{0:T(128)} %weights_hbm.1, s32[1,192]{1,0:T(1,128)} %bitcast.2, s32[192,128]{1,0:T(8,128)} %row_hbm.1, s32[192,128]{1,0:T(8,128)} %col_hbm.1, f32[192,128,128]{2,1,0:T(8,128)} %a_hbm.1), custom_call_target="tpu_custom_call" | custom-call | tf_op jit(solution)/shard_map/coarse_blocks/pallas_call | solution.py:356
  37.5 0.7 %finish.1 = (f32[8,32,128]{2,1,0:T(8,128)}, s32[1,8]{1,0:T(1,128)}) custom-call(f32[32,8,128]{2,1,0:T(8,128)S(1)} %get-tuple-element.6.back, s32[1,128]{1,0:T(1,128)S(1)} %get-tuple-element.7.note), custom_call_target="tpu_custom_call" | custom-call | tf_op jit(solution)/shard_map/finish/pallas_call | solution.py:393
